TPU v7x, 128 devices: a whole 4x4x4 slice. The times are simulated.
128 devices in a mesh: dp: 1, sp: 128 (over z, y, x, core).
Axes of the slice: x: 4, y: 4, z: 4, core: 2. Of those that a mesh axis runs over, the one named last changes fastest.
Arguments:
- tokens: bfloat16 [128, 2048], P('dp')
- w_query: bfloat16 [2048, 2048], replicated
- w_key: bfloat16 [2048, 256], replicated
- w_value: bfloat16 [2048, 256], replicated
- w_out: bfloat16 [2048, 2048], P('sp')
- k_cache: bfloat16 [128, 4096, 256], P('dp', 'sp')
- v_cache: bfloat16 [128, 4096, 256], P('dp', 'sp')
- positions: int32 [128], P('dp')
Outputs:
- output 1: bfloat16 [128, 2048], P('dp')
- output 2: bfloat16 [128, 4096, 256], P('dp', 'sp')
- output 3: bfloat16 [128, 4096, 256], P('dp', 'sp')
All inputs are finite; a program needn't handle non-finite values.
Results may differ from a plain program's by a relative error of at most 0.00402255.
Values are sent between devices in bfloat16 or wider.
A program may use at most 1 GiB of HBM per device.

v0:
```python
import jax
import jax.numpy as jnp
from jax import lax
from jax.sharding import PartitionSpec as P


def solution(mesh):
    def local_step(tokens, w_query, w_key, w_value, w_out, k_cache, v_cache, positions):
        n_rows, seq_local, head_dim = k_cache.shape
        q_width = w_query.shape[1]
        n_heads = q_width // head_dim
        rows_local = w_out.shape[0]
        shard_idx = lax.axis_index('sp')
        queries = jnp.dot(tokens, w_query, preferred_element_type=jnp.float32).astype(jnp.bfloat16).reshape(n_rows, n_heads, head_dim)
        key_new = jnp.dot(tokens, w_key, preferred_element_type=jnp.float32).astype(jnp.bfloat16)
        value_new = jnp.dot(tokens, w_value, preferred_element_type=jnp.float32).astype(jnp.bfloat16)
        local_pos = positions - shard_idx * seq_local
        slot_ids = jnp.arange(seq_local)
        hit_mask = (slot_ids[None, :] == local_pos[:, None])[:, :, None]
        k_upd = jnp.where(hit_mask, key_new[:, None, :], k_cache)
        v_upd = jnp.where(hit_mask, value_new[:, None, :], v_cache)
        scores = jnp.einsum('bhd,btd->bht', queries, k_upd, preferred_element_type=jnp.float32) * head_dim ** -0.5
        valid_mask = (slot_ids[None, :] <= local_pos[:, None])[:, None, :]
        scores = jnp.where(valid_mask, scores, -jnp.inf)
        row_peak = jnp.maximum(jnp.max(scores, axis=2), -1e30)
        weights = jnp.exp(scores - row_peak[:, :, None])
        weight_sum = jnp.sum(weights, axis=2)
        value_sum = jnp.einsum('bht,btd->bhd', weights.astype(jnp.bfloat16), v_upd, preferred_element_type=jnp.float32)
        peak_all = lax.pmax(row_peak, 'sp')
        rescale = jnp.exp(row_peak - peak_all)
        weight_all = lax.psum(weight_sum * rescale, 'sp')
        value_all = lax.psum(value_sum * rescale[:, :, None], 'sp')
        attn_heads = (value_all / weight_all[:, :, None]).astype(jnp.bfloat16).reshape(n_rows, q_width)
        attn_local = lax.dynamic_slice_in_dim(attn_heads, shard_idx * rows_local, rows_local, axis=1)
        partial = jnp.dot(attn_local, w_out, preferred_element_type=jnp.float32)
        attn_out = lax.psum(partial, 'sp').astype(jnp.bfloat16)
        return attn_out, k_upd, v_upd

    cache_spec = P('dp', 'sp', None)
    return jax.shard_map(local_step, mesh=mesh, in_specs=(P('dp', None), P(), P(), P(), P('sp', None), cache_spec, cache_spec, P('dp')), out_specs=(P('dp', None), cache_spec, cache_spec), check_vma=False)
```

profile of v0, /device:TPU:1, one launch (start us, length us, event | category | flops | bytes accessed | tf_op | source)
XLA Modules:
  0.0 320.1 jit_solution(16009281554635428965)
XLA Ops:
  7.2 0.0 copy-start
  7.2 0.0 copy-start.2
  7.2 0.0 all-reduce.3.cloned.1.call-start
  7.2 0.8 broadcast_subtract_fusion
  8.0 0.1 iota_compare_fusion.1
  8.1 0.3 copy-done
  8.4 1.3 convolution_convert_fusion.2
  9.8 1.7 convolution_convert_fusion.1
  11.5 0.0 copy-done.2
  11.5 0.0 copy-start.3
  11.5 0.0 copy-start.4
  11.5 4.8 %convolution_convert_fusion = bf16[128,2048]{1,0:T(8,128)(2,1)S(1)} fusion(bf16[128,2048]{1,0:T(8,128)(2,1)S(1)} %copy-done.2, bf16[2048,2048]{1,0:T(8,128)(2,1)} %param.9), kind=kOutput, calls=%fused_computation | convolution fusion | flops 1074003968 | bytes 9437184 | tf_op jit(solution)/shard_map/dot_general | solution.py:14
  16.3 0.1 copy.11
  16.4 0.0 copy-done.3
  16.4 0.0 copy-done.4
  16.4 2.3 broadcast_select_fusion.1
  18.7 0.0 copy-start.1
  18.7 1.5 fusion.9
  20.2 69.0 %pmax.7 = f32[128,8]{1,0:T(8,128)S(1)} all-reduce(f32[128,8]{1,0:T(8,128)S(1)} %broadcast_maximum_fusion), channel_id=1, replica_groups=mesh['dp'=1,'sp'=128] {'sp'}, use_global_device_ids=true, to_apply=%region_1.2 | all-reduce | flops 1024 | bytes 8192 | tf_op jit(solution)/shard_map/pmax | solution.py:29
  89.2 1.4 fusion.1
  90.7 0.0 copy-done.1
  90.7 3.3 %convolution_multiply_fusion = f32[128,8,256]{2,1,0:T(8,128)} fusion(bf16[128,32,256]{2,1,0:T(8,128)(2,1)} %get-tuple-element.6, f32[128,8]{1,0:T(8,128)S(1)} %get-tuple-element.4, f32[128,8,32]{2,1,0:T(8,128)} %get-tuple-element.10, f32[128,8]{1,0:T(8,128)S(1)} %broadcast_maximum_fusion), kind=kOutput, calls=%fused_computation.3 | convolution fusion | flops 17104896 | bytes 3284992 | tf_op jit(solution)/shard_map/bht,btd->bhd/dot_general | solution.py:28
  93.9 0.0 copy-start.5
  93.9 0.0 all-reduce.3.cloned.1.call-update
  94.0 63.0 %psum.22 = f32[128,8]{1,0:T(8,128)S(1)} all-reduce(f32[128,8]{1,0:T(8,128)S(1)} %get-tuple-element.3), channel_id=1, replica_groups=mesh['dp'=1,'sp'=128] {'sp'}, use_global_device_ids=true, to_apply=%region_4.5 | all-reduce | flops 1024 | bytes 8192 | tf_op jit(solution)/shard_map/psum | solution.py:31
  157.0 83.4 %all-reduce.3.cloned.1.call-done = f32[128,8,256]{2,1,0:T(8,128)} async-done(((f32[128,8,256]{2,1,0:T(8,128)}), f32[128,8,256]{2,1,0:T(8,128)}) %all-reduce.3.cloned.1.call-update) | async-done | bytes 1048592 | tf_op jit(solution)/shard_map/psum | solution.py:32
  240.4 1.4 divide_convert_fusion
  241.8 0.1 copy.12
  241.9 0.0 copy-done.5
  241.9 0.3 fusion.5
  242.3 71.0 %all-reduce.4 = bf16[128,2048]{1,0:T(8,128)(2,1)} all-reduce(f32[128,2048]{1,0:T(8,128)S(1)} %fusion.5), channel_id=1, replica_groups=mesh['dp'=1,'sp'=128] {'sp'}, use_global_device_ids=true, to_apply=%region_5.6 | all-reduce | flops 262144 | bytes 1572864 | tf_op jit(solution)/shard_map/psum | solution.py:36
  (2 shorter events, 0.0 us)
Async XLA Ops:
  7.2 1.2 copy-start
  7.2 4.3 %copy-start.2 = (bf16[128,2048]{1,0:T(8,128)(2,1)S(1)}, bf16[128,2048]{1,0:T(8,128)(2,1)}, u32[]{:S(2)}) copy-start(bf16[128,2048]{1,0:T(8,128)(2,1)} %param.8) | copy-start | bytes 1572868
  7.2 233.2 %all-reduce.3.cloned.1.call-start = ((), (), s32[]{:S(2)}) async-start(), calls=%async_computation | async-start | bytes 2097152 | tf_op jit(solution)/shard_map/psum | solution.py:32
  11.5 4.9 %copy-start.3 = (bf16[128,32,256]{2,1,0:T(8,128)(2,1)S(1)}, bf16[128,32,256]{2,1,0:T(8,128)(2,1)}, u32[]{:S(2)}) copy-start(bf16[128,32,256]{2,1,0:T(8,128)(2,1)} %param.13) | copy-start | bytes 6291460
  11.5 4.9 %copy-start.4 = (bf16[128,32,256]{2,1,0:T(8,128)(2,1)S(1)}, bf16[128,32,256]{2,1,0:T(8,128)(2,1)}, u32[]{:S(2)}) copy-start(bf16[128,32,256]{2,1,0:T(8,128)(2,1)} %param.14) | copy-start | bytes 6291460
  18.7 71.9 %copy-start.1 = (bf16[128,32,256]{2,1,0:T(8,128)(2,1)}, bf16[128,32,256]{2,1,0:T(8,128)(2,1)S(1)}, u32[]{:S(2)}) copy-start(bf16[128,32,256]{2,1,0:T(8,128)(2,1)S(1)} %get-tuple-element.5) | copy-start | bytes 6291460
  93.9 148.0 %copy-start.5 = (bf16[16,2048]{1,0:T(8,128)(2,1)S(1)}, bf16[16,2048]{1,0:T(8,128)(2,1)}, u32[]{:S(2)}) copy-start(bf16[16,2048]{1,0:T(8,128)(2,1)} %param.12) | copy-start | bytes 196612
Sparse Core Ops, SparseCore 0:
  94.1 146.2 all-reduce.2
where the time goes:
time: 321 us; the launch traced here: 320 us
  blocking collectives  203 us (63%)
  waiting for transfers between devices  83.4 us (26%)
  between operations  14.2 us (4%)
  matrix products  12.9 us (4%)
  other arithmetic  6.01 us (2%)
    psum x1, waiting for transfers between devices, local_step(): value_all = lax.psum(value_sum * rescale[:, :, None], 'sp')  83.4 us
    psum x1, blocking collectives, local_step(): attn_out = lax.psum(partial, 'sp').astype(jnp.bfloat16)  71 us
    pmax x1, blocking collectives, local_step(): peak_all = lax.pmax(row_peak, 'sp')  69 us
    psum x1, blocking collectives, local_step(): weight_all = lax.psum(weight_sum * rescale, 'sp')  63 us
  transfers between devices with their start and end apart: 1, of which 1 were waited for; matrix products, arithmetic and copies ran while one was open for 0% of the time, Pallas kernels for 0%

commit v1 on v0

v1 whole, which is shorter than its diff:
```python
import jax
import jax.numpy as jnp
from jax import lax
from jax.experimental import pallas as pl
from jax.experimental.pallas import tpu as pltpu
from jax.sharding import PartitionSpec as P

F32 = jnp.float32
BF16 = jnp.bfloat16
SIDE = 4
MESH = pl.DeviceIdType.MESH
LOWEST = float(jnp.finfo(jnp.float32).min)


def attention_kernel(pos_ref, q_ref, k_ref, v_ref, wo_ref, out_ref,
                     qs, own, r0, s1, r1, s2, r2, s3, r3, osc, w1, wo_all, y_all,
                     d0_s, d0_r, wz_s, wz_r, wg_s, wg_r, s1_s, s1_r, s2_s, s2_r, s3_s, s3_r,
                     o_s, o_r, yz_s, yz_r, yg_s, yg_r, yd_s, yd_r):
    me = lax.axis_index('sp')
    c = lax.rem(me, 2)
    x = lax.rem(me // 2, SIDE)
    y = lax.rem(me // 8, SIDE)
    z = me // 32
    base = me * 32

    def dev(zz, yy, xx, cc):
        return {'sp': ((zz * SIDE + yy) * SIDE + xx) * 2 + cc}

    def fwd(a, d):
        return lax.rem(a + d, SIDE)

    mate = dev(z, y, x, 1 - c)
    x_peer = [None] + [dev(z, y, fwd(x, d), c) for d in (1, 2, 3)]
    y_peer = [None] + [dev(z, fwd(y, d), x, c) for d in (1, 2, 3)]
    z_peer = [None] + [dev(fwd(z, d), y, x, c) for d in (1, 2, 3)]

    barrier = pltpu.get_barrier_semaphore()
    for peer in [mate] + x_peer[1:] + y_peer[1:] + z_peer[1:]:
        pl.semaphore_signal(barrier, inc=1, device_id=peer, device_id_type=MESH)

    def rcopy(src, dst, ssem, rsem, peer):
        return pltpu.make_async_remote_copy(src_ref=src, dst_ref=dst, send_sem=ssem, recv_sem=rsem,
                                            device_id=peer, device_id_type=MESH)

    for h in range(8):
        qh = q_ref[:, h * 256:(h + 1) * 256].astype(F32).reshape(16, 8, 256)
        qs[:, h] = qh

    pl.semaphore_wait(barrier, 10)

    pend = []
    w_mate = rcopy(wo_ref.at[:, pl.ds(pl.multiple_of((1 - c) * 1024, 1024), 1024)], w1, wz_s.at[6], wz_r.at[6], mate)
    w_mate.start()
    wz = []
    for d in (1, 2, 3):
        zz = fwd(z, d)
        cp = rcopy(wo_ref.at[:, pl.ds(pl.multiple_of(c * 1024 + zz * 256, 256), 256)], wo_all.at[z, y, x, c],
                   wz_s.at[d - 1], wz_r.at[d - 1], z_peer[d])
        cp.start()
        wz.append(cp)
    wo_all[z, y, x, c] = wo_ref[:, pl.ds(pl.multiple_of(c * 1024 + z * 256, 256), 256)]

    lane = lax.broadcasted_iota(jnp.int32, (8, 128), 1)
    sub256 = lax.broadcasted_iota(jnp.int32, (8, 256), 0)
    col_t = lax.broadcasted_iota(jnp.int32, (8, 256), 1) - 32 * sub256

    def tile_of(r):
        gy = fwd(y, 1 + r // SIDE)
        gx = fwd(x, 1 + lax.rem(r, SIDE))
        return gy, gx

    def d0_copy(r, g):
        return rcopy(own.at[g, 1 - c], r0.at[g], d0_s.at[r], d0_r.at[r], mate)

    def attend(r):
        gy, gx = tile_of(r)
        g = gy * SIDE + gx
        kg = k_ref[pl.ds(g * 8, 8)].reshape(256, 256)
        vg = v_ref[pl.ds(g * 8, 8)].reshape(256, 256)
        qg = qs[g].reshape(64, 256).astype(BF16)
        s = lax.dot_general(qg, kg, (((1,), (1,)), ((), ())), preferred_element_type=F32) * 0.0625
        lim = jnp.zeros((8, 256), jnp.int32)
        for j in range(8):
            lim = jnp.where(sub256 == j, pos_ref[g * 8 + j] - base, lim)
        valid = (col_t >= 0) & (col_t < 32) & (col_t <= lim)
        s = jnp.where(valid[None], s.reshape(8, 8, 256), -jnp.inf)
        m = jnp.maximum(jnp.max(s, axis=2, keepdims=True), LOWEST)
        w = jnp.exp(s - m)
        l = jnp.sum(w, axis=2, keepdims=True)
        o = jnp.dot(w.astype(BF16).reshape(64, 256), vg, preferred_element_type=F32).reshape(8, 8, 256)
        for half in range(2):
            for st in range(2):
                h0 = half * 4 + st * 2
                for j in range(2):
                    for k in range(2):
                        own[g, half, st, 2 * j + k] = o[h0 + j, :, k * 128:(k + 1) * 128]
                own[g, half, st, 4] = jnp.where(lane == 0, m[h0], jnp.where(lane == 1, m[h0 + 1], jnp.where(
                    lane == 2, l[h0], l[h0 + 1])))
        d0_copy(r, g).start()

    def combine(parts):
        stats = [p[4] for p in parts]
        top = stats[0]
        for t in stats[1:]:
            top = jnp.maximum(top, t)
        data = [None] * 4
        total = None
        for p, t in zip(parts, stats):
            a = jnp.exp(t - top)
            f = [jnp.broadcast_to(a[:, j:j + 1], (8, 128)) for j in range(2)]
            for i in range(4):
                term = p[i] * f[i // 2]
                data[i] = term if data[i] is None else data[i] + term
            term = t * jnp.where(lane % 2 == 0, f[0], f[1])
            total = term if total is None else total + term
        return data, top, total

    def put(dst, parts):
        data, top, total = combine(parts)
        for i in range(4):
            dst[i] = data[i]
        dst[4] = jnp.where(lane < 2, top, total)

    def s1_copy(st, d, g, idx, peer):
        return rcopy(s1.at[g, st], r1.at[st, d - 1, idx], s1_s.at[st, d - 1, idx], s1_r.at[st, d - 1, idx], peer)

    def finish(r):
        gy, gx = tile_of(r)
        g = gy * SIDE + gx
        d0_copy(r, g).wait_recv()
        for st in range(2):
            put(s1.at[g, st], [own.at[g, c, st], r0.at[g, st]])

        @pl.when(lax.rem(r, SIDE) < SIDE - 1)
        def _():
            s1_copy(0, 1 + lax.rem(r, SIDE), g, gy, dev(z, y, gx, c)).start()

        @pl.when(r // SIDE < SIDE - 1)
        def _():
            s1_copy(1, 1 + r // SIDE, g, gx, dev(z, gy, x, c)).start()

    LAG = 3

    def step(r, carry):
        @pl.when(r < 16)
        def _():
            attend(r)

        @pl.when(r >= LAG)
        def _():
            finish(r - LAG)
        return carry

    lax.fori_loop(0, 8, step, 0)

    w_mate.wait_recv()
    for d in (1, 2, 3):
        zz = fwd(z, d)
        cp = rcopy(w1.at[:, pl.ds(pl.multiple_of(zz * 256, 256), 256)], wo_all.at[z, y, x, 1 - c],
                   wz_s.at[2 + d], wz_r.at[2 + d], z_peer[d])
        cp.start()
        wz.append(cp)
    wo_all[z, y, x, 1 - c] = w1[:, pl.ds(pl.multiple_of(z * 256, 256), 256)]

    lax.fori_loop(8, 16 + LAG, step, 0)

    for cp in wz:
        cp.wait_recv()
    wg1, wg2 = [], []
    for d in (1, 2, 3):
        for st, peer in ((0, x_peer[d]), (1, y_peer[d])):
            cp = rcopy(wo_all.at[:, y, x, st], wo_all.at[:, y, x, st], wg_s.at[0, st, d - 1], wg_r.at[0, st, d - 1], peer)
            cp.start()
            wg1.append(cp)

    s2c = []
    for d in (1, 2, 3, 0):
        for st in range(2):
            idx = fwd(y, d) if st == 0 else fwd(x, d)
            g = idx * SIDE + x if st == 0 else y * SIDE + idx
            for e in (1, 2, 3):
                s1_copy(st, e, g, idx, mate).wait_recv()
            put(s2.at[st, idx], [s1.at[g, st]] + [r1.at[st, e, idx] for e in range(3)])
            if d:
                cp = rcopy(s2.at[st, idx], r2.at[st, d - 1], s2_s.at[st, d - 1], s2_r.at[st, d - 1],
                           (y_peer if st == 0 else x_peer)[d])
                cp.start()
                s2c.append((st, d, cp))

    for cp in wg1:
        cp.wait_recv()
    for d in (1, 2, 3):
        for st, peer in ((0, y_peer[d]), (1, x_peer[d])):
            ref = wo_all.at[:, y, :, 0] if st == 0 else wo_all.at[:, :, x, 1]
            cp = rcopy(ref, ref, wg_s.at[1, st, d - 1], wg_r.at[1, st, d - 1], peer)
            cp.start()
            wg2.append(cp)

    s3c = []
    for st in range(2):
        for s, _, cp in s2c:
            if s == st:
                cp.wait_recv()
        put(s3.at[st], [s2.at[st, y if st == 0 else x]] + [r2.at[st, e] for e in range(3)])
        for d in (1, 2, 3):
            cp = rcopy(s3.at[st], r3.at[st, d - 1], s3_s.at[st, d - 1], s3_r.at[st, d - 1], z_peer[d])
            cp.start()
            s3c.append((st, cp))
    for st in range(2):
        for s, cp in s3c:
            if s == st:
                cp.wait_recv()
        data, _, total = combine([s3.at[st]] + [r3.at[st, e] for e in range(3)])
        for j in range(2):
            den = jnp.broadcast_to(total[:, 2 + j:3 + j], (8, 128))
            for k in range(2):
                osc[c, 2 * st + j, :, k * 128:(k + 1) * 128] = (data[2 * j + k] / den).astype(BF16)
    ocp = rcopy(osc.at[c], osc.at[c], o_s, o_r, mate)
    ocp.start()
    for cp in wg2:
        cp.wait_recv()
    ocp.wait_recv()

    acc = jnp.zeros((8, 256), F32)
    for h in range(8):
        wh = wo_all[h // 2, 2 * (h % 2):2 * (h % 2) + 2].reshape(256, 256)
        acc = acc + jnp.dot(osc[h // 4, h % 4], wh, preferred_element_type=F32)
    y_all[c, y, x, z] = acc.astype(BF16)

    yzc = []
    for d in (1, 2, 3):
        ref = y_all.at[c, y, x, z]
        cp = rcopy(ref, ref, yz_s.at[d - 1], yz_r.at[d - 1], z_peer[d])
        cp.start()
        yzc.append(cp)
    for cp in yzc:
        cp.wait_recv()
    yg, ydc = {}, []

    def half(st):
        return pl.ds(2 * st, 2)

    for d in (1, 2, 3):
        for st, peer in ((0, x_peer[d]), (1, y_peer[d])):
            ref = y_all.at[c, y, x, half(st)]
            cp = rcopy(ref, ref, yg_s.at[0, st, d - 1], yg_r.at[0, st, d - 1], peer)
            cp.start()
            yg[0, st, d] = cp
    for st in range(2):
        for d in (1, 2, 3):
            yg[0, st, d].wait_recv()
        ref = y_all.at[c, y, :, half(0)] if st == 0 else y_all.at[c, :, x, half(1)]
        for d in (1, 2, 3):
            cp = rcopy(ref, ref, yg_s.at[1, st, d - 1], yg_r.at[1, st, d - 1], (y_peer if st == 0 else x_peer)[d])
            cp.start()
            yg[1, st, d] = cp
        cp = rcopy(ref, ref, yd_s.at[st, 0], yd_r.at[st, 0], mate)
        cp.start()
        ydc.append(cp)
    for d in (1, 2, 3):
        for st in range(2):
            yg[1, st, d].wait_recv()
            if st == 0:
                ref = y_all.at[c, fwd(y, 4 - d), :, half(0)]
            else:
                ref = y_all.at[c, :, fwd(x, 4 - d), half(1)]
            cp = rcopy(ref, ref, yd_s.at[st, d], yd_r.at[st, d], mate)
            cp.start()
            ydc.append(cp)
    for cp in ydc:
        cp.wait_recv()
    out_ref[...] = y_all[...]

    def drain0(r, carry):
        gy, gx = tile_of(r)
        d0_copy(r, gy * SIDE + gx).wait_send()
        return carry

    lax.fori_loop(0, 16, drain0, 0)
    for d in (1, 2, 3):
        for idx in range(4):
            s1_copy(0, d, idx * SIDE + fwd(x, d), idx, mate).wait_send()
            s1_copy(1, d, fwd(y, d) * SIDE + idx, idx, mate).wait_send()
    for cp in [w_mate] + wz + wg1 + wg2 + [t[2] for t in s2c] + [t[1] for t in s3c] + [ocp] + yzc + list(yg.values()) + ydc:
        cp.wait_send()


def solution(mesh):
    def local_step(tokens, w_query, w_key, w_value, w_out, k_cache, v_cache, positions):
        n_rows, seq_local, head_dim = k_cache.shape
        shard_idx = lax.axis_index('sp')
        queries = jnp.dot(tokens, w_query, preferred_element_type=F32).astype(BF16)
        key_new = jnp.dot(tokens, w_key, preferred_element_type=F32).astype(BF16)
        value_new = jnp.dot(tokens, w_value, preferred_element_type=F32).astype(BF16)
        local_pos = positions - shard_idx * seq_local
        hit_mask = (jnp.arange(seq_local)[None, :] == local_pos[:, None])[:, :, None]
        k_upd = jnp.where(hit_mask, key_new[:, None, :], k_cache)
        v_upd = jnp.where(hit_mask, value_new[:, None, :], v_cache)
        vm = pl.BlockSpec(memory_space=pltpu.VMEM)
        msg = (5, 8, 128)
        dma = pltpu.SemaphoreType.DMA
        blocks = pl.pallas_call(
            attention_kernel,
            out_shape=jax.ShapeDtypeStruct((2, 4, 4, 4, 8, 256), BF16),
            in_specs=[pl.BlockSpec(memory_space=pltpu.SMEM), vm, vm, vm, vm],
            out_specs=vm,
            scratch_shapes=[
                pltpu.VMEM((16, 8, 8, 256), F32),
                pltpu.VMEM((16, 2, 2) + msg, F32),
                pltpu.VMEM((16, 2) + msg, F32),
                pltpu.VMEM((16, 2) + msg, F32),
                pltpu.VMEM((2, 3, 4) + msg, F32),
                pltpu.VMEM((2, 4) + msg, F32),
                pltpu.VMEM((2, 3) + msg, F32),
                pltpu.VMEM((2,) + msg, F32),
                pltpu.VMEM((2, 3) + msg, F32),
                pltpu.VMEM((2, 4, 8, 256), BF16),
                pltpu.VMEM((16, 1024), BF16),
                pltpu.VMEM((4, 4, 4, 2, 16, 256), BF16),
                pltpu.VMEM((2, 4, 4, 4, 8, 256), BF16),
                dma((16,)), dma((16,)), dma((7,)), dma((7,)), dma((2, 2, 3)), dma((2, 2, 3)),
                dma((2, 3, 4)), dma((2, 3, 4)), dma((2, 3)), dma((2, 3)), dma((2, 3)), dma((2, 3)),
                dma, dma, dma((3,)), dma((3,)), dma((2, 2, 3)), dma((2, 2, 3)), dma((2, 4)), dma((2, 4)),
            ],
            compiler_params=pltpu.CompilerParams(collective_id=0, has_side_effects=True,
                                                 vmem_limit_bytes=40 * 1024 * 1024),
        )(positions, queries, k_upd, v_upd, w_out)
        attn_out = blocks.transpose(1, 2, 4, 0, 3, 5).reshape(n_rows, 2048)
        return attn_out, k_upd, v_upd

    cache_spec = P('dp', 'sp', None)
    return jax.shard_map(local_step, mesh=mesh, in_specs=(P('dp', None), P(), P(), P(), P('sp', None), cache_spec, cache_spec, P('dp')), out_specs=(P('dp', None), cache_spec, cache_spec), check_vma=False)
```

time: 321 us -> 56.5 us (0.18)
  blocking collectives: 203 us -> 0 us
  waiting for transfers between devices: 83.4 us -> 0 us
  Pallas kernels: 0 us -> 44.1 us
  between operations: 14.2 us -> 0.81 us
  matrix products: 12.9 us -> 7.83 us
  other arithmetic: 6.01 us -> 1.78 us
    psum x2 -> x0, blocking collectives: 134 us -> none  [the longest x1 71 us: local_step(): attn_out = lax.psum(partial, 'sp').astype(jnp.bfloat16)]
    psum x1 -> x0, waiting for transfers between devices: 83.4 us -> none  [local_step(): value_all = lax.psum(value_sum * rescale[:, :, None], 'sp')]
    pmax x1 -> x0, blocking collectives: 69 us -> none  [local_step(): peak_all = lax.pmax(row_peak, 'sp')]
    pallas_call x0 -> x1, Pallas kernels: none -> 44.1 us  [local_step(): pl.pallas_call(attention_kernel, out_shape=jax.ShapeDtypeStruct((2, 4, 4,...]
    dot_general x6 -> x3, matrix products: 12.9 us -> 7.83 us  [the longest x1 4.79 us: local_step(): queries = jnp.dot(tokens, w_query, preferred_element_type=F32).astype(BF16)]
  transfers between devices with their start and end apart: 1 -> 0, of which waited for: 1 -> 0; matrix products, arithmetic and copies ran while one was open for 0% -> 0% of each run, Pallas kernels for 0% -> 0%
where the time goes in v1:
time: 56.5 us; the launch traced here: 56.4 us
  Pallas kernels  44.1 us (78%)
  matrix products  7.83 us (14%)
  local copies, waits for them, and re-layouts  1.82 us (3%)
  other arithmetic  1.78 us (3%)
  between operations  0.81 us (1%)
    pallas_call x1, Pallas kernels, local_step(): pl.pallas_call(attention_kernel, out_shape=jax.ShapeDtypeStruct((2, 4, 4,...  44.1 us
    dot_general x1, matrix products, local_step(): queries = jnp.dot(tokens, w_query, preferred_element_type=F32).astype(BF16)  4.79 us
    dot_general x1, matrix products, local_step(): jnp.dot(tokens, w_value, preferred_element_type=F32).astype(BF16)  1.7 us
    dot_general x1, matrix products, local_step(): key_new = jnp.dot(tokens, w_key, preferred_element_type=F32).astype(BF16)  1.35 us
    reshape x1, local copies, waits for them, and re-layouts, local_step(): attn_out = blocks.transpose(1, 2, 4, 0, 3, 5).reshape(n_rows, 2048)  1.18 us

profile of v1, /device:TPU:1, one launch (start us, length us, event | category | flops | bytes accessed | tf_op | source)
XLA Modules:
  0.0 56.4 jit_solution(16912221623647023071)
XLA Ops:
  0.6 0.0 copy-start
  0.6 0.0 copy-start.5
  0.7 0.8 %broadcast_subtract_fusion = s32[128]{0:T(128)S(1)} fusion(s32[128]{0:T(128)} %pos_ref.1, s32[]{:T(128)S(6)} %mul.3), kind=kLoop, calls=%fused_computation.6 | loop fusion | flops 128 | bytes 1028 | tf_op jit(solution)/shard_map/sub | solution.py:295
  1.4 0.1 iota_compare_fusion
  1.5 0.3 copy-done
  1.9 1.3 %convolution_convert_fusion.2 = bf16[128,256]{1,0:T(8,128)(2,1)S(1)} fusion(bf16[128,2048]{1,0:T(8,128)(2,1)} %param.8, bf16[2048,256]{1,0:T(8,128)(2,1)S(1)} %copy-done), kind=kOutput, calls=%fused_computation.4 | convolution fusion | flops 134250496 | bytes 1638400 | tf_op jit(solution)/shard_map/dot_general | solution.py:293
  3.2 1.7 %convolution_convert_fusion.1 = bf16[128,256]{1,0:T(8,128)(2,1)S(1)} fusion(bf16[128,2048]{1,0:T(8,128)(2,1)} %param.8, bf16[2048,256]{1,0:T(8,128)(2,1)} %param.11), kind=kOutput, calls=%fused_computation.3 | convolution fusion | flops 134250496 | bytes 1638400 | tf_op jit(solution)/shard_map/dot_general | solution.py:294
  4.9 0.0 copy-done.5
  4.9 0.0 copy-start.6
  5.0 0.0 copy-start.7
  5.0 4.8 %convolution_convert_fusion.q_ref = bf16[128,2048]{1,0:T(8,128)(2,1)S(1)} fusion(bf16[128,2048]{1,0:T(8,128)(2,1)S(1)} %copy-done.5, bf16[2048,2048]{1,0:T(8,128)(2,1)} %param.9), kind=kOutput, calls=%fused_computation | convolution fusion | flops 1074003968 | bytes 9437184 | tf_op jit(solution)/shard_map/dot_general | solution.py:292
  9.8 0.0 copy-done.6
  9.8 0.0 copy-done.7
  9.8 0.0 copy-start.3
  9.8 0.0 copy-start.4
  9.8 0.9 %broadcast_select_fusion = (bf16[128,32,256]{2,1,0:T(8,128)(2,1)S(1)}, bf16[128,32,256]{2,1,0:T(8,128)(2,1)S(1)}) fusion(bf16[128,32,256]{2,1,0:T(8,128)(2,1)S(1)} %copy-done.6, pred[128,32]{1,0:T(8,128)(4,1)S(1)} %iota_compare_fusion, bf16[128,256]{1,0:T(8,128)(2,1)S(1)} %convolution_convert_fusion.1, bf16[128,32,256]{2,1,0:T(8,128)(2,1)S(1)} %copy-done.7, ...), kind=kLoop, calls=%fused_computation.1 | loop fusion | flops 2097152 | bytes 8523776 | tf_op jit(solution)/shard_map/jit(_where)/select_n | solution.py:298
  10.7 0.0 copy-start.1
  10.7 0.0 copy-start.2
  10.8 0.0 copy-done.3
  10.8 0.0 copy-done.4
  10.8 44.1 %shard_map.103 = bf16[2,4,4,4,8,256]{5,4,3,2,1,0:T(8,128)(2,1)S(1)} custom-call(s32[128]{0:T(128)S(1)} %copy-done.4, bf16[128,2048]{1,0:T(8,128)(2,1)S(1)} %convolution_convert_fusion.q_ref, bf16[128,32,256]{2,1,0:T(8,128)(2,1)S(1)} %get-tuple-element.4.k_ref, bf16[128,32,256]{2,1,0:T(8,128)(2,1)S(1)} %get-tuple-element.3.v_ref, bf16[16,2048]{1,0:T(8,128)(2,1)S(1)} %copy-done.3), custom_call_target="tpu_custom_call" | custom-call | tf_op jit(solution)/shard_map/pallas_call | solution.py:302
  54.9 0.0 copy-done.1
  54.9 0.0 copy-done.2
  54.9 0.2 copy.11
  55.2 1.2 %reshape.32 = bf16[128,2048]{1,0:T(8,128)(2,1)} reshape(bf16[4,4,8,2,4,256]{5,4,3,2,1,0:T(4,128)(2,1)S(1)} %copy.11) | data formatting | bytes 1048576 | tf_op jit(solution)/shard_map/reshape | solution.py:328
Async XLA Ops:
  0.6 1.2 %copy-start = (bf16[2048,256]{1,0:T(8,128)(2,1)S(1)}, bf16[2048,256]{1,0:T(8,128)(2,1)}, u32[]{:S(2)}) copy-start(bf16[2048,256]{1,0:T(8,128)(2,1)} %param.10) | copy-start | bytes 3145732
  0.6 4.3 %copy-start.5 = (bf16[128,2048]{1,0:T(8,128)(2,1)S(1)}, bf16[128,2048]{1,0:T(8,128)(2,1)}, u32[]{:S(2)}) copy-start(bf16[128,2048]{1,0:T(8,128)(2,1)} %param.8) | copy-start | bytes 1572868
  4.9 4.8 %copy-start.6 = (bf16[128,32,256]{2,1,0:T(8,128)(2,1)S(1)}, bf16[128,32,256]{2,1,0:T(8,128)(2,1)}, u32[]{:S(2)}) copy-start(bf16[128,32,256]{2,1,0:T(8,128)(2,1)} %param.14) | copy-start | bytes 6291460
  5.0 4.8 %copy-start.7 = (bf16[128,32,256]{2,1,0:T(8,128)(2,1)S(1)}, bf16[128,32,256]{2,1,0:T(8,128)(2,1)}, u32[]{:S(2)}) copy-start(bf16[128,32,256]{2,1,0:T(8,128)(2,1)} %param.13) | copy-start | bytes 6291460
  9.8 1.0 %copy-start.3 = (bf16[16,2048]{1,0:T(8,128)(2,1)S(1)}, bf16[16,2048]{1,0:T(8,128)(2,1)}, u32[]{:S(2)}) copy-start(bf16[16,2048]{1,0:T(8,128)(2,1)} %wo_ref.1) | copy-start | bytes 196612
  9.8 1.0 %copy-start.4 = (s32[128]{0:T(128)S(1)}, s32[128]{0:T(128)}, u32[]{:S(2)}) copy-start(s32[128]{0:T(128)} %pos_ref.1) | copy-start | bytes 1540
  10.7 44.2 %copy-start.1 = (bf16[128,32,256]{2,1,0:T(8,128)(2,1)}, bf16[128,32,256]{2,1,0:T(8,128)(2,1)S(1)}, u32[]{:S(2)}) copy-start(bf16[128,32,256]{2,1,0:T(8,128)(2,1)S(1)} %get-tuple-element.3.v_ref) | copy-start | bytes 6291460
  10.7 44.2 %copy-start.2 = (bf16[128,32,256]{2,1,0:T(8,128)(2,1)}, bf16[128,32,256]{2,1,0:T(8,128)(2,1)S(1)}, u32[]{:S(2)}) copy-start(bf16[128,32,256]{2,1,0:T(8,128)(2,1)S(1)} %get-tuple-element.4.k_ref) | copy-start | bytes 6291460
